TPU v7x, 32 devices: a whole 2x2x4 slice. The times are simulated.
32 devices in a mesh: row: 8 (over z, x), col: 4 (over y, core).
Axes of the slice: x: 2, y: 2, z: 4, core: 2. Of those that a mesh axis runs over, the one named last changes fastest.
Arguments:
- eigvecs: float32 [2048, 512], P('row', 'col'), may hold values from -6 to 6
- reflectors: float32 [8, 32, 128, 64], P(None, ('row', 'col')), may hold values from -2 to 2, as said below
- factors: float32 [8, 32, 64, 64], P(None, ('row', 'col')), may hold values from -3 to 3, as said below
- order: int32 [8], replicated, may hold values from 0 to 7, each once
- offsets: int32 [8], replicated, may hold values from 0 to 63
Outputs:
- rotated: float32 [2048, 512], P('row', 'col')
Inputs may be any that keep to these rules, and one draw needn't show every extreme that they name: `order`: a permutation of 0 .. 7. Every block map is orthogonal: with V the block of reflectors and T the block of factors, T is upper triangular and T^-1 + T^-T = V^T V. `factors`: upper triangular, paired with reflectors as promised there.
All inputs are finite; a program needn't handle non-finite values.
Results may differ from a plain program's by a relative error of at most 0.0003.
Values sent between devices are 32-bit elements; how exact they have to be, the bound alone decides.
A program may use at most 64 MiB of HBM per device.

v0:
```python
import jax
import jax.numpy as jnp
from jax import lax
from jax.sharding import PartitionSpec as P

highest = lax.Precision.HIGHEST


def passed_along(block, axis, distance):
    devices = range(lax.axis_size(axis))
    route = [(i - distance, i) for i in devices if i - distance in devices]
    return lax.ppermute(block, axis, route)


def entering(array, axis, combine, identity):
    size, position = (lax.axis_size(axis), lax.axis_index(axis))
    everything = jax.tree.map(lambda part: lax.all_gather(part, axis), array)
    start = jax.tree.map(
        lambda part, zero: jnp.broadcast_to(jnp.asarray(zero, part.dtype), part.shape),
        array,
        identity,
    )

    def hop(k, before):
        reached = k < position
        new = combine(before, jax.tree.map(lambda part: part[k], everything))
        return jax.tree.map(lambda a, b: jnp.where(reached, a, b), new, before)

    return lax.fori_loop(0, size, hop, start)


def reflect(segment, householder, triangle):
    inner = jnp.dot(householder.T, segment, precision=highest, preferred_element_type=jnp.float32)
    inner = jnp.dot(triangle, inner, precision=highest, preferred_element_type=jnp.float32)
    return segment - jnp.dot(
        householder, inner, precision=highest, preferred_element_type=jnp.float32
    )


def sweep_apply(extended, house_set, tri_set, offset):
    block_width = house_set.shape[-1]

    def advance(number, current):
        start = offset + number * block_width
        segment = lax.dynamic_slice_in_dim(current, start, 2 * block_width, 0)
        householder = lax.dynamic_index_in_dim(house_set, number, 0, keepdims=False)
        triangle = lax.dynamic_index_in_dim(tri_set, number, 0, keepdims=False)
        return lax.dynamic_update_slice_in_dim(
            current, reflect(segment, householder, triangle), start, 0
        )

    return lax.fori_loop(0, house_set.shape[0], advance, extended)


def compose(earlier, later):
    first_map = jnp.dot(later[0], earlier[0], precision=highest, preferred_element_type=jnp.float32)
    shifted = (
        jnp.dot(later[0], earlier[1], precision=highest, preferred_element_type=jnp.float32)
        + later[1]
    )
    return (first_map, shifted)


def local(eigvecs, reflectors, factors, order, offsets):
    height = eigvecs.shape[0]
    columns = eigvecs.shape[1]
    block_width = reflectors.shape[-1]
    span_rows = 2 * block_width
    leading = lax.axis_index("row") == 0
    identity = jnp.eye(span_rows, dtype=jnp.float32)
    probe = jnp.concatenate([identity, jnp.zeros((height, span_rows), jnp.float32)], 0)
    vectors = eigvecs
    for position in range(order.shape[0]):
        stored = order[position]
        offset = offsets[stored]
        own_house = lax.dynamic_index_in_dim(reflectors, stored, 0, keepdims=False)
        own_tri = lax.dynamic_index_in_dim(factors, stored, 0, keepdims=False)
        house_set, tri_set = (
            lax.all_gather(own_house, "col", axis=0, tiled=True),
            lax.all_gather(own_tri, "col", axis=0, tiled=True),
        )
        next_rows = passed_along(vectors[:span_rows], "row", -1)
        top_rows = jnp.where(leading, vectors[:span_rows], 0.0)
        extended = jnp.concatenate([top_rows, vectors[span_rows:], next_rows], 0)
        joined = sweep_apply(jnp.concatenate([extended, probe], 1), house_set, tri_set, offset)
        partial_value = joined[:, :columns]
        response = joined[:, columns:]
        transfer = jnp.where(leading, 0.0, response[height:])
        empty = jnp.zeros((span_rows, columns), jnp.float32)
        composed = entering((transfer, partial_value[height:]), "row", compose, (identity, empty))
        incoming = composed[1]
        vectors = partial_value[:height] + jnp.dot(
            response[:height], incoming, precision=highest, preferred_element_type=jnp.float32
        )
    return vectors


def solution(mesh):
    placed = (
        P("row", "col"),
        P(None, ("row", "col"), None, None),
        P(None, ("row", "col"), None, None),
        P(),
        P(),
    )
    return jax.shard_map(
        local, mesh=mesh, in_specs=placed, out_specs=P("row", "col"), check_vma=False
    )
```

profile of v0, /device:TPU:0, one launch (start us, length us, event | category | flops | bytes accessed | tf_op | source)
XLA Modules:
  0.0 719.6 jit_solution(1707958535803900348)
XLA Ops:
  0.9 1.3 collective-permute-start
  21.1 6.5 all-gather.1
  27.6 5.6 all-gather
  33.2 9.2 %while.216 = (s32[]{:T(128)}, f32[384,256]{1,0:T(8,128)S(1)}, s32[]{:T(128)}, f32[4,128,64]{1,2,0:T(8,128)S(1)}, f32[4,64,64]{2,1,0:T(8,128)S(1)}, /*index=5*/s32[]{:T(128)}, s32[]{:T(128)}, s32[]{:T(128)}, s32[]{:T(128)}) while((s32[]{:T(128)}, f32[384,256]{1,0:T(8,128)S(1)}, s32[]{:T(128)}, f32[4,128,64]{1,2,0:T(8,128)S(1)}, ...), condition=%wide.region_1.2_spmd, body=%wide.region_0.1_spmd.sunk | while | flops 62947336 | bytes 1015983 | solution.py:52
  34.6 1.0 dynamic_update_slice.64
  37.1 1.0 dynamic_update_slice.64
  42.5 34.1 %all-gather.2 = f32[1024,128]{1,0:T(8,128)S(1)} all-gather(f32[128,128]{1,0:T(8,128)S(1)} %get-tuple-element.1884), channel_id=4, replica_groups=mesh['row'=8,'col'=4] {'row'}, dimensions={0}, use_global_device_ids=true | all-gather | bytes 589824 | tf_op jit(solution)/shard_map/all_gather | solution.py:17
  76.6 31.2 %all-gather.3 = f32[1024,128]{1,0:T(8,128)S(1)} all-gather(f32[128,128]{1,0:T(8,128)S(1)} %get-tuple-element.1883), channel_id=5, replica_groups=mesh['row'=8,'col'=4] {'row'}, dimensions={0}, use_global_device_ids=true | all-gather | bytes 589824 | tf_op jit(solution)/shard_map/all_gather | solution.py:17
  107.7 2.0 while.224
  110.0 1.3 collective-permute-start.1
  111.3 5.4 all-gather.5
  116.7 5.4 all-gather.4
  122.2 9.4 %while.217 = (s32[]{:T(128)}, f32[384,256]{1,0:T(8,128)S(1)}, s32[]{:T(128)}, f32[4,128,64]{1,2,0:T(8,128)S(1)}, f32[4,64,64]{2,1,0:T(8,128)S(1)}, /*index=5*/s32[]{:T(128)}, s32[]{:T(128)}, s32[]{:T(128)}, s32[]{:T(128)}) while((s32[]{:T(128)}, f32[384,256]{1,0:T(8,128)S(1)}, s32[]{:T(128)}, f32[4,128,64]{1,2,0:T(8,128)S(1)}, ...), condition=%wide.region_5.6_spmd, body=%wide.region_4.5_spmd.sunk | while | flops 62947336 | bytes 1015983 | solution.py:52
  123.6 1.0 dynamic_update_slice.65
  126.1 1.0 dynamic_update_slice.65
  131.6 31.7 %all-gather.6 = f32[1024,128]{1,0:T(8,128)S(1)} all-gather(f32[128,128]{1,0:T(8,128)S(1)} %get-tuple-element.1882), channel_id=8, replica_groups=mesh['row'=8,'col'=4] {'row'}, dimensions={0}, use_global_device_ids=true | all-gather | bytes 589824 | tf_op jit(solution)/shard_map/all_gather | solution.py:17
  163.3 31.4 %all-gather.7 = f32[1024,128]{1,0:T(8,128)S(1)} all-gather(f32[128,128]{1,0:T(8,128)S(1)} %get-tuple-element.1881), channel_id=9, replica_groups=mesh['row'=8,'col'=4] {'row'}, dimensions={0}, use_global_device_ids=true | all-gather | bytes 589824 | tf_op jit(solution)/shard_map/all_gather | solution.py:17
  194.6 2.0 while.225
  196.9 1.3 collective-permute-start.2
  198.2 5.4 all-gather.9
  203.7 5.4 all-gather.8
  209.1 9.1 %while.218 = (s32[]{:T(128)}, f32[384,256]{1,0:T(8,128)S(1)}, s32[]{:T(128)}, f32[4,128,64]{1,2,0:T(8,128)S(1)}, f32[4,64,64]{2,1,0:T(8,128)S(1)}, /*index=5*/s32[]{:T(128)}, s32[]{:T(128)}, s32[]{:T(128)}, s32[]{:T(128)}) while((s32[]{:T(128)}, f32[384,256]{1,0:T(8,128)S(1)}, s32[]{:T(128)}, f32[4,128,64]{1,2,0:T(8,128)S(1)}, ...), condition=%wide.region_9.10_spmd, body=%wide.region_8.9_spmd.sunk | while | flops 62947336 | bytes 1015983 | solution.py:52
  210.5 1.0 dynamic_update_slice.66
  212.9 1.0 dynamic_update_slice.66
  218.2 31.8 %all-gather.10 = f32[1024,128]{1,0:T(8,128)S(1)} all-gather(f32[128,128]{1,0:T(8,128)S(1)} %get-tuple-element.1880), channel_id=12, replica_groups=mesh['row'=8,'col'=4] {'row'}, dimensions={0}, use_global_device_ids=true | all-gather | bytes 589824 | tf_op jit(solution)/shard_map/all_gather | solution.py:17
  250.0 31.5 %all-gather.11 = f32[1024,128]{1,0:T(8,128)S(1)} all-gather(f32[128,128]{1,0:T(8,128)S(1)} %get-tuple-element.1879), channel_id=13, replica_groups=mesh['row'=8,'col'=4] {'row'}, dimensions={0}, use_global_device_ids=true | all-gather | bytes 589824 | tf_op jit(solution)/shard_map/all_gather | solution.py:17
  281.5 2.0 while.226
  283.8 1.3 collective-permute-start.3
  285.1 5.4 all-gather.13
  290.5 5.4 all-gather.12
  295.9 9.5 %while.219 = (s32[]{:T(128)}, f32[384,256]{1,0:T(8,128)S(1)}, s32[]{:T(128)}, f32[4,128,64]{1,2,0:T(8,128)S(1)}, f32[4,64,64]{2,1,0:T(8,128)S(1)}, /*index=5*/s32[]{:T(128)}, s32[]{:T(128)}, s32[]{:T(128)}, s32[]{:T(128)}) while((s32[]{:T(128)}, f32[384,256]{1,0:T(8,128)S(1)}, s32[]{:T(128)}, f32[4,128,64]{1,2,0:T(8,128)S(1)}, ...), condition=%wide.region_13.14_spmd, body=%wide.region_12.13_spmd.sunk | while | flops 62947336 | bytes 1015983 | solution.py:52
  297.4 1.0 dynamic_update_slice.67
  305.5 31.9 %all-gather.14 = f32[1024,128]{1,0:T(8,128)S(1)} all-gather(f32[128,128]{1,0:T(8,128)S(1)} %get-tuple-element.1878), channel_id=16, replica_groups=mesh['row'=8,'col'=4] {'row'}, dimensions={0}, use_global_device_ids=true | all-gather | bytes 589824 | tf_op jit(solution)/shard_map/all_gather | solution.py:17
  337.3 31.5 %all-gather.15 = f32[1024,128]{1,0:T(8,128)S(1)} all-gather(f32[128,128]{1,0:T(8,128)S(1)} %get-tuple-element.1877), channel_id=17, replica_groups=mesh['row'=8,'col'=4] {'row'}, dimensions={0}, use_global_device_ids=true | all-gather | bytes 589824 | tf_op jit(solution)/shard_map/all_gather | solution.py:17
  368.8 2.0 while.227
  371.1 1.3 collective-permute-start.4
  372.4 5.4 all-gather.17
  377.8 5.4 all-gather.16
  383.3 9.3 %while.220 = (s32[]{:T(128)}, f32[384,256]{1,0:T(8,128)S(1)}, s32[]{:T(128)}, f32[4,128,64]{1,2,0:T(8,128)S(1)}, f32[4,64,64]{2,1,0:T(8,128)S(1)}, /*index=5*/s32[]{:T(128)}, s32[]{:T(128)}, s32[]{:T(128)}, s32[]{:T(128)}) while((s32[]{:T(128)}, f32[384,256]{1,0:T(8,128)S(1)}, s32[]{:T(128)}, f32[4,128,64]{1,2,0:T(8,128)S(1)}, ...), condition=%wide.region_17.18_spmd, body=%wide.region_16.17_spmd.sunk | while | flops 62947336 | bytes 1015983 | solution.py:52
  384.7 1.0 dynamic_update_slice.68
  392.6 31.6 %all-gather.18 = f32[1024,128]{1,0:T(8,128)S(1)} all-gather(f32[128,128]{1,0:T(8,128)S(1)} %get-tuple-element.1876), channel_id=20, replica_groups=mesh['row'=8,'col'=4] {'row'}, dimensions={0}, use_global_device_ids=true | all-gather | bytes 589824 | tf_op jit(solution)/shard_map/all_gather | solution.py:17
  424.2 31.3 %all-gather.19 = f32[1024,128]{1,0:T(8,128)S(1)} all-gather(f32[128,128]{1,0:T(8,128)S(1)} %get-tuple-element.1875), channel_id=21, replica_groups=mesh['row'=8,'col'=4] {'row'}, dimensions={0}, use_global_device_ids=true | all-gather | bytes 589824 | tf_op jit(solution)/shard_map/all_gather | solution.py:17
  455.5 2.0 while.228
  457.8 1.3 collective-permute-start.5
  459.1 5.4 all-gather.21
  464.5 5.4 all-gather.20
  470.0 9.6 %while.221 = (s32[]{:T(128)}, f32[384,256]{1,0:T(8,128)S(1)}, s32[]{:T(128)}, f32[4,128,64]{1,2,0:T(8,128)S(1)}, f32[4,64,64]{2,1,0:T(8,128)S(1)}, /*index=5*/s32[]{:T(128)}, s32[]{:T(128)}, s32[]{:T(128)}, s32[]{:T(128)}) while((s32[]{:T(128)}, f32[384,256]{1,0:T(8,128)S(1)}, s32[]{:T(128)}, f32[4,128,64]{1,2,0:T(8,128)S(1)}, ...), condition=%wide.region_21.22_spmd, body=%wide.region_20.21_spmd.sunk | while | flops 62947336 | bytes 1015983 | solution.py:52
  479.6 31.8 %all-gather.22 = f32[1024,128]{1,0:T(8,128)S(1)} all-gather(f32[128,128]{1,0:T(8,128)S(1)} %get-tuple-element.1874), channel_id=24, replica_groups=mesh['row'=8,'col'=4] {'row'}, dimensions={0}, use_global_device_ids=true | all-gather | bytes 589824 | tf_op jit(solution)/shard_map/all_gather | solution.py:17
  511.4 31.4 %all-gather.23 = f32[1024,128]{1,0:T(8,128)S(1)} all-gather(f32[128,128]{1,0:T(8,128)S(1)} %get-tuple-element.1873), channel_id=25, replica_groups=mesh['row'=8,'col'=4] {'row'}, dimensions={0}, use_global_device_ids=true | all-gather | bytes 589824 | tf_op jit(solution)/shard_map/all_gather | solution.py:17
  542.7 2.0 while.229
  545.0 1.3 collective-permute-start.6
  546.3 5.6 all-gather.25
  551.9 5.4 all-gather.24
  557.4 9.3 %while.222 = (s32[]{:T(128)}, f32[384,256]{1,0:T(8,128)S(1)}, s32[]{:T(128)}, f32[4,128,64]{1,2,0:T(8,128)S(1)}, f32[4,64,64]{2,1,0:T(8,128)S(1)}, /*index=5*/s32[]{:T(128)}, s32[]{:T(128)}, s32[]{:T(128)}, s32[]{:T(128)}) while((s32[]{:T(128)}, f32[384,256]{1,0:T(8,128)S(1)}, s32[]{:T(128)}, f32[4,128,64]{1,2,0:T(8,128)S(1)}, ...), condition=%wide.region_25.26_spmd, body=%wide.region_24.25_spmd.sunk | while | flops 62947336 | bytes 1015983 | solution.py:52
  566.6 31.6 %all-gather.26 = f32[1024,128]{1,0:T(8,128)S(1)} all-gather(f32[128,128]{1,0:T(8,128)S(1)} %get-tuple-element.1872), channel_id=28, replica_groups=mesh['row'=8,'col'=4] {'row'}, dimensions={0}, use_global_device_ids=true | all-gather | bytes 589824 | tf_op jit(solution)/shard_map/all_gather | solution.py:17
  598.3 31.4 %all-gather.27 = f32[1024,128]{1,0:T(8,128)S(1)} all-gather(f32[128,128]{1,0:T(8,128)S(1)} %get-tuple-element.1871), channel_id=29, replica_groups=mesh['row'=8,'col'=4] {'row'}, dimensions={0}, use_global_device_ids=true | all-gather | bytes 589824 | tf_op jit(solution)/shard_map/all_gather | solution.py:17
  629.7 2.0 while.230
  632.0 1.3 collective-permute-start.7
  633.3 5.4 all-gather.29
  638.7 5.4 all-gather.28
  644.1 9.2 %while.223 = (s32[]{:T(128)}, f32[384,256]{1,0:T(8,128)S(1)}, s32[]{:T(128)}, f32[4,128,64]{1,2,0:T(8,128)S(1)}, f32[4,64,64]{2,1,0:T(8,128)S(1)}, /*index=5*/s32[]{:T(128)}, s32[]{:T(128)}, s32[]{:T(128)}, s32[]{:T(128)}) while((s32[]{:T(128)}, f32[384,256]{1,0:T(8,128)S(1)}, s32[]{:T(128)}, f32[4,128,64]{1,2,0:T(8,128)S(1)}, ...), condition=%wide.region_29.30_spmd, body=%wide.region_28.29_spmd.sunk | while | flops 62947336 | bytes 1015983 | solution.py:52
  653.4 31.8 %all-gather.30 = f32[1024,128]{1,0:T(8,128)S(1)} all-gather(f32[128,128]{1,0:T(8,128)S(1)} %get-tuple-element.1870), channel_id=32, replica_groups=mesh['row'=8,'col'=4] {'row'}, dimensions={0}, use_global_device_ids=true | all-gather | bytes 589824 | tf_op jit(solution)/shard_map/all_gather | solution.py:17
  685.2 31.5 %all-gather.31 = f32[1024,128]{1,0:T(8,128)S(1)} all-gather(f32[128,128]{1,0:T(8,128)S(1)} %get-tuple-element.1869), channel_id=33, replica_groups=mesh['row'=8,'col'=4] {'row'}, dimensions={0}, use_global_device_ids=true | all-gather | bytes 589824 | tf_op jit(solution)/shard_map/all_gather | solution.py:17
  716.7 2.0 while.231
  (310 shorter events, 65.0 us)
Async XLA Ops:
  0.0 18.8 %copy-start = (f32[8,1,128,64]{2,3,1,0:T(8,128)S(1)}, f32[8,1,128,64]{2,3,1,0:T(8,128)}, u32[]{:S(2)}) copy-start(f32[8,1,128,64]{2,3,1,0:T(8,128)} %param.38) | copy-start | bytes 786436
  0.9 1.3 copy-start.3
  0.9 32.3 %collective-permute-start = (f32[128,128]{1,0:T(8,128)S(1)}, f32[128,128]{1,0:T(8,128)S(1)}, u32[]{:S(2)}, u32[]{:S(2)}) collective-permute-start(f32[128,128]{1,0:T(8,128)S(1)} %get-tuple-element.1924), channel_id=1, source_target_pairs={{4,0},{8,4},{12,8},{16,12},{20,16},{24,20},{28,24},{5,1},{9,5},{13... | collective-permute-start | bytes 196616 | tf_op jit(solution)/shard_map/ppermute | solution.py:12
  18.8 1.0 copy-start.1
  19.7 0.7 copy-start.2
  110.0 12.1 %collective-permute-start.1 = (f32[128,128]{1,0:T(8,128)S(1)}, f32[128,128]{1,0:T(8,128)S(1)}, u32[]{:S(2)}, u32[]{:S(2)}) collective-permute-start(f32[128,128]{1,0:T(8,128)S(1)} %get-tuple-element.1921), channel_id=1, source_target_pairs={{4,0},{8,4},{12,8},{16,12},{20,16},{24,20},{28,24},{5,1},{9,5},{13... | collective-permute-start | bytes 196616 | tf_op jit(solution)/shard_map/ppermute | solution.py:12
  196.9 12.1 %collective-permute-start.2 = (f32[128,128]{1,0:T(8,128)S(1)}, f32[128,128]{1,0:T(8,128)S(1)}, u32[]{:S(2)}, u32[]{:S(2)}) collective-permute-start(f32[128,128]{1,0:T(8,128)S(1)} %get-tuple-element.1918), channel_id=1, source_target_pairs={{4,0},{8,4},{12,8},{16,12},{20,16},{24,20},{28,24},{5,1},{9,5},{13... | collective-permute-start | bytes 196616 | tf_op jit(solution)/shard_map/ppermute | solution.py:12
  283.8 12.1 %collective-permute-start.3 = (f32[128,128]{1,0:T(8,128)S(1)}, f32[128,128]{1,0:T(8,128)S(1)}, u32[]{:S(2)}, u32[]{:S(2)}) collective-permute-start(f32[128,128]{1,0:T(8,128)S(1)} %get-tuple-element.1915), channel_id=1, source_target_pairs={{4,0},{8,4},{12,8},{16,12},{20,16},{24,20},{28,24},{5,1},{9,5},{13... | collective-permute-start | bytes 196616 | tf_op jit(solution)/shard_map/ppermute | solution.py:12
  371.1 12.1 %collective-permute-start.4 = (f32[128,128]{1,0:T(8,128)S(1)}, f32[128,128]{1,0:T(8,128)S(1)}, u32[]{:S(2)}, u32[]{:S(2)}) collective-permute-start(f32[128,128]{1,0:T(8,128)S(1)} %get-tuple-element.1912), channel_id=1, source_target_pairs={{4,0},{8,4},{12,8},{16,12},{20,16},{24,20},{28,24},{5,1},{9,5},{13... | collective-permute-start | bytes 196616 | tf_op jit(solution)/shard_map/ppermute | solution.py:12
  457.8 12.1 %collective-permute-start.5 = (f32[128,128]{1,0:T(8,128)S(1)}, f32[128,128]{1,0:T(8,128)S(1)}, u32[]{:S(2)}, u32[]{:S(2)}) collective-permute-start(f32[128,128]{1,0:T(8,128)S(1)} %get-tuple-element.1909), channel_id=1, source_target_pairs={{4,0},{8,4},{12,8},{16,12},{20,16},{24,20},{28,24},{5,1},{9,5},{13... | collective-permute-start | bytes 196616 | tf_op jit(solution)/shard_map/ppermute | solution.py:12
  545.0 12.3 %collective-permute-start.6 = (f32[128,128]{1,0:T(8,128)S(1)}, f32[128,128]{1,0:T(8,128)S(1)}, u32[]{:S(2)}, u32[]{:S(2)}) collective-permute-start(f32[128,128]{1,0:T(8,128)S(1)} %get-tuple-element.1906), channel_id=1, source_target_pairs={{4,0},{8,4},{12,8},{16,12},{20,16},{24,20},{28,24},{5,1},{9,5},{13... | collective-permute-start | bytes 196616 | tf_op jit(solution)/shard_map/ppermute | solution.py:12
  632.0 12.1 %collective-permute-start.7 = (f32[128,128]{1,0:T(8,128)S(1)}, f32[128,128]{1,0:T(8,128)S(1)}, u32[]{:S(2)}, u32[]{:S(2)}) collective-permute-start(f32[128,128]{1,0:T(8,128)S(1)} %get-tuple-element.1903), channel_id=1, source_target_pairs={{4,0},{8,4},{12,8},{16,12},{20,16},{24,20},{28,24},{5,1},{9,5},{13... | collective-permute-start | bytes 196616 | tf_op jit(solution)/shard_map/ppermute | solution.py:12
where the time goes:
time: 721 us; the launch traced here: 720 us
  blocking collectives  595 us (83%)
  matrix products  39.6 us (5%)
  local copies, waits for them, and re-layouts  31.9 us (4%)
  loops' own time  24.8 us (3%)
  between operations  16.3 us (2%)
  starting transfers between devices  10.3 us (1%)
    all_gather x16, blocking collectives, entering(): everything = jax.tree.map(lambda part: lax.all_gather(part, axis), array)  507 us
    all_gather x8, blocking collectives, local(): lax.all_gather(own_tri, 'col', axis=0, tiled=True)  44.6 us
    all_gather x8, blocking collectives, local(): lax.all_gather(own_house, 'col', axis=0, tiled=True)  43.4 us
    dynamic_update_slice x32, local copies, waits for them, and re-layouts, advance(): lax.dynamic_update_slice_in_dim(current, reflect(segment, householder, tr...  28.6 us
    another operation x8, loops' own time, sweep_apply(): return lax.fori_loop(0, house_set.shape[0], advance, extended)  22.6 us
  transfers between devices with their start and end apart: 8, of which 0 were waited for; matrix products, arithmetic and copies ran while one was open for 0% of the time, Pallas kernels for 0%

commit v1 on v0

--- a/solution.py
+++ b/solution.py
@@ -4,6 +4,27 @@
 from jax.sharding import PartitionSpec as P
 
 highest = lax.Precision.HIGHEST
+
+
+def ring_gather(x, axis, dim):
+    size, index, rows = (lax.axis_size(axis), lax.axis_index(axis), x.shape[dim])
+    upward = [(i, (i + 1) % size) for i in range(size)]
+    backward = [(i, (i - 1) % size) for i in range(size)]
+    filled = jnp.zeros((*x.shape[:dim], size * rows, *x.shape[dim + 1 :]), x.dtype)
+    filled = lax.dynamic_update_slice_in_dim(filled, x, index * rows, axis=dim)
+    from_left = from_right = x
+    halfway = size // 2
+    for step in range(1, halfway + 1):
+        from_left = lax.ppermute(from_left, axis, upward)
+        filled = lax.dynamic_update_slice_in_dim(
+            filled, from_left, (index - step) % size * rows, axis=dim
+        )
+        if step < size - halfway:
+            from_right = lax.ppermute(from_right, axis, backward)
+            filled = lax.dynamic_update_slice_in_dim(
+                filled, from_right, (index + step) % size * rows, axis=dim
+            )
+    return filled
 
 
 def passed_along(block, axis, distance):
@@ -76,7 +97,7 @@
         own_house = lax.dynamic_index_in_dim(reflectors, stored, 0, keepdims=False)
         own_tri = lax.dynamic_index_in_dim(factors, stored, 0, keepdims=False)
         house_set, tri_set = (
-            lax.all_gather(own_house, "col", axis=0, tiled=True),
+            ring_gather(own_house, "col", 0),
             lax.all_gather(own_tri, "col", axis=0, tiled=True),
         )
         next_rows = passed_along(vectors[:span_rows], "row", -1)

time: 721 us -> 793 us (1.100)
  matrix products: 39.6 us -> 81.1 us
  blocking collectives: 595 us -> 560 us
  waiting for transfers between devices: 0.02 us -> 29.1 us
  starting transfers between devices: 10.3 us -> 28.8 us
  local copies, waits for them, and re-layouts: 31.9 us -> 49.7 us
    all_gather x8 -> x0, blocking collectives: 43.4 us -> none  [local(): lax.all_gather(own_house, 'col', axis=0, tiled=True)]
    ppermute x8, waiting for transfers between devices: 0.02 us -> 29 us  [passed_along(): return lax.ppermute(block, axis, route)]
    dot_general x32, matrix products: 6.26 us -> 27.5 us  [reflect(): jnp.dot(triangle, inner, precision=highest, preferred_element_type=jnp.fl...]
    dot_general x64, matrix products: 13.4 us -> 33.9 us  [compose(): jnp.dot(later[0], earlier[1], precision=highest, preferred_element_type=j...]
    ppermute x0 -> x24, starting transfers between devices: none -> 18.3 us  [the longest x8 13.3 us: ring_gather(): from_right = lax.ppermute(from_right, axis, backward)]
    dynamic_update_slice x0 -> x32, local copies, waits for them, and re-layouts: none -> 14.6 us  [the longest x16 12.7 us: ring_gather(): lax.dynamic_update_slice_in_dim(filled, from_left, (index - step) % size...]
  transfers between devices with their start and end apart: 8 -> 32, of which waited for: 0 -> 8; matrix products, arithmetic and copies ran while one was open for 0% -> 15% of each run, Pallas kernels for 0% -> 0%
where the time goes in v1:
time: 793 us; the launch traced here: 789 us
  blocking collectives  560 us (71%)
  matrix products  81.1 us (10%)
  local copies, waits for them, and re-layouts  49.7 us (6%)
  waiting for transfers between devices  29.1 us (4%)
  starting transfers between devices  28.8 us (4%)
  loops' own time  23.3 us (3%)
  between operations  16 us (2%)
    all_gather x16, blocking collectives, entering(): everything = jax.tree.map(lambda part: lax.all_gather(part, axis), array)  512 us
    all_gather x8, blocking collectives, local(): lax.all_gather(own_tri, 'col', axis=0, tiled=True)  47.1 us
    dot_general x64, matrix products, compose(): jnp.dot(later[0], earlier[1], precision=highest, preferred_element_type=j...  33.9 us
    ppermute x8, waiting for transfers between devices, passed_along(): return lax.ppermute(block, axis, route)  29 us
    dynamic_update_slice x32, local copies, waits for them, and re-layouts, advance(): lax.dynamic_update_slice_in_dim(current, reflect(segment, householder, tr...  28.6 us
    dot_general x32, matrix products, reflect(): jnp.dot(triangle, inner, precision=highest, preferred_element_type=jnp.fl...  27.5 us
    another operation x8, loops' own time, sweep_apply(): return lax.fori_loop(0, house_set.shape[0], advance, extended)  21.1 us
  transfers between devices with their start and end apart: 32, of which 8 were waited for; matrix products, arithmetic and copies ran while one was open for 15% of the time, Pallas kernels for 0%

profile of v1, /device:TPU:0, one launch (start us, length us, event | category | flops | bytes accessed | tf_op | source)
XLA Modules:
  0.0 788.6 jit_solution(1463450017836296087)
XLA Ops:
  0.0 1.6 fusion.185
  18.3 2.0 collective-permute-start.2
  23.6 6.3 all-gather
  30.0 5.9 all-gather.3
  35.9 5.9 all-gather.6
  41.9 5.9 all-gather.9
  47.8 5.9 all-gather.12
  53.8 5.9 all-gather.15
  61.4 5.9 all-gather.18
  68.7 5.6 all-gather.21
  74.3 1.3 collective-permute-start.10
  77.4 1.8 collective-permute-start.14
  80.9 1.8 collective-permute-start.18
  83.6 1.8 collective-permute-start.22
  86.3 1.8 collective-permute-start.26
  89.0 1.8 collective-permute-start.30
  91.7 1.3 collective-permute-start
  95.7 1.4 collective-permute-start.15
  98.2 12.0 %while.216 = (s32[]{:T(128)}, f32[384,256]{1,0:T(8,128)S(1)}, s32[]{:T(128)}, f32[4,128,64]{2,1,0:T(8,128)S(1)}, f32[4,64,64]{2,1,0:T(8,128)}, /*index=5*/s32[]{:T(128)}, s32[]{:T(128)}, s32[]{:T(128)}, s32[]{:T(128)}) while((s32[]{:T(128)}, f32[384,256]{1,0:T(8,128)S(1)}, s32[]{:T(128)}, f32[4,128,64]{2,1,0:T(8,128)S(1)}, ...), condition=%wide.region_1.2_spmd, body=%wide.region_0.1_spmd.sunk | while | flops 62947336 | bytes 1082027 | solution.py:73
  110.2 35.9 %all-gather.1 = f32[1024,128]{1,0:T(8,128)} all-gather(f32[128,128]{1,0:T(8,128)S(1)} %get-tuple-element.1844), channel_id=3, replica_groups=mesh['row'=8,'col'=4] {'row'}, dimensions={0}, use_global_device_ids=true | all-gather | bytes 589824 | tf_op jit(solution)/shard_map/all_gather | solution.py:38
  146.1 33.5 %all-gather.2 = f32[1024,128]{1,0:T(8,128)} all-gather(f32[128,128]{1,0:T(8,128)S(1)} %get-tuple-element.1843), channel_id=4, replica_groups=mesh['row'=8,'col'=4] {'row'}, dimensions={0}, use_global_device_ids=true | all-gather | bytes 589824 | tf_op jit(solution)/shard_map/all_gather | solution.py:38
  179.6 9.0 %while.224 = (s32[]{:T(128)}, f32[128,128]{1,0:T(8,128)S(1)}, s32[]{:T(128)}, f32[8,128,128]{2,1,0:T(8,128)}, f32[8,128,128]{2,1,0:T(8,128)}, /*index=5*/s32[]{:T(128)}, s32[]{:T(128)}) while((s32[]{:T(128)}, f32[128,128]{1,0:T(8,128)S(1)}, s32[]{:T(128)}, f32[8,128,128]{2,1,0:T(8,128)}, f32[8,128,128]{2,1,0:T(8,128)}, ...), condition=%wide.region_3.4_spmd.clone, body=%wide.region_2.3_spmd.clone.sunk | while | flops 25231364 | bytes 461407 | solution.py:50
  188.9 1.3 collective-permute-start.4
  191.0 4.0 collective-permute-done.4
  195.1 11.9 %while.217 = (s32[]{:T(128)}, f32[384,256]{1,0:T(8,128)S(1)}, s32[]{:T(128)}, f32[4,128,64]{2,1,0:T(8,128)S(1)}, f32[4,64,64]{2,1,0:T(8,128)}, /*index=5*/s32[]{:T(128)}, s32[]{:T(128)}, s32[]{:T(128)}, s32[]{:T(128)}) while((s32[]{:T(128)}, f32[384,256]{1,0:T(8,128)S(1)}, s32[]{:T(128)}, f32[4,128,64]{2,1,0:T(8,128)S(1)}, ...), condition=%wide.region_5.6_spmd, body=%wide.region_4.5_spmd.sunk | while | flops 62947336 | bytes 1082027 | solution.py:73
  207.0 31.7 %all-gather.4 = f32[1024,128]{1,0:T(8,128)S(1)} all-gather(f32[128,128]{1,0:T(8,128)S(1)} %get-tuple-element.1842), channel_id=6, replica_groups=mesh['row'=8,'col'=4] {'row'}, dimensions={0}, use_global_device_ids=true | all-gather | bytes 589824 | tf_op jit(solution)/shard_map/all_gather | solution.py:38
  238.7 33.5 %all-gather.5 = f32[1024,128]{1,0:T(8,128)} all-gather(f32[128,128]{1,0:T(8,128)S(1)} %get-tuple-element.1841), channel_id=7, replica_groups=mesh['row'=8,'col'=4] {'row'}, dimensions={0}, use_global_device_ids=true | all-gather | bytes 589824 | tf_op jit(solution)/shard_map/all_gather | solution.py:38
  272.2 8.7 %while.225 = (s32[]{:T(128)}, f32[128,128]{1,0:T(8,128)S(1)}, s32[]{:T(128)}, f32[8,128,128]{2,1,0:T(8,128)S(1)}, f32[8,128,128]{2,1,0:T(8,128)}, /*index=5*/s32[]{:T(128)}, s32[]{:T(128)}) while((s32[]{:T(128)}, f32[128,128]{1,0:T(8,128)S(1)}, s32[]{:T(128)}, f32[8,128,128]{2,1,0:T(8,128)S(1)}, f32[8,128,128]{2,1,0:T(8,128)}, ...), condition=%wide.region_7.8_spmd.clone, body=%wide.region_6.7_spmd.clone.sunk | while | flops 25231364 | bytes 461407 | solution.py:50
  281.3 1.3 collective-permute-start.8
  283.4 4.0 collective-permute-done.8
  287.5 12.1 %while.218 = (s32[]{:T(128)}, f32[384,256]{1,0:T(8,128)S(1)}, s32[]{:T(128)}, f32[4,128,64]{2,1,0:T(8,128)S(1)}, f32[4,64,64]{2,1,0:T(8,128)}, /*index=5*/s32[]{:T(128)}, s32[]{:T(128)}, s32[]{:T(128)}, s32[]{:T(128)}) while((s32[]{:T(128)}, f32[384,256]{1,0:T(8,128)S(1)}, s32[]{:T(128)}, f32[4,128,64]{2,1,0:T(8,128)S(1)}, ...), condition=%wide.region_9.10_spmd, body=%wide.region_8.9_spmd.sunk | while | flops 62947336 | bytes 1082027 | solution.py:73
  299.6 31.5 %all-gather.7 = f32[1024,128]{1,0:T(8,128)S(1)} all-gather(f32[128,128]{1,0:T(8,128)S(1)} %get-tuple-element.1840), channel_id=9, replica_groups=mesh['row'=8,'col'=4] {'row'}, dimensions={0}, use_global_device_ids=true | all-gather | bytes 589824 | tf_op jit(solution)/shard_map/all_gather | solution.py:38
  331.1 33.4 %all-gather.8 = f32[1024,128]{1,0:T(8,128)} all-gather(f32[128,128]{1,0:T(8,128)S(1)} %get-tuple-element.1839), channel_id=10, replica_groups=mesh['row'=8,'col'=4] {'row'}, dimensions={0}, use_global_device_ids=true | all-gather | bytes 589824 | tf_op jit(solution)/shard_map/all_gather | solution.py:38
  364.5 8.7 %while.226 = (s32[]{:T(128)}, f32[128,128]{1,0:T(8,128)S(1)}, s32[]{:T(128)}, f32[8,128,128]{2,1,0:T(8,128)S(1)}, f32[8,128,128]{2,1,0:T(8,128)}, /*index=5*/s32[]{:T(128)}, s32[]{:T(128)}) while((s32[]{:T(128)}, f32[128,128]{1,0:T(8,128)S(1)}, s32[]{:T(128)}, f32[8,128,128]{2,1,0:T(8,128)S(1)}, f32[8,128,128]{2,1,0:T(8,128)}, ...), condition=%wide.region_11.12_spmd.clone, body=%wide.region_10.11_spmd.clone.sunk | while | flops 25231364 | bytes 461407 | solution.py:50
  373.6 1.3 collective-permute-start.12
  375.7 4.0 collective-permute-done.12
  379.7 12.3 %while.219 = (s32[]{:T(128)}, f32[384,256]{1,0:T(8,128)S(1)}, s32[]{:T(128)}, f32[4,128,64]{2,1,0:T(8,128)S(1)}, f32[4,64,64]{2,1,0:T(8,128)}, /*index=5*/s32[]{:T(128)}, s32[]{:T(128)}, s32[]{:T(128)}, s32[]{:T(128)}) while((s32[]{:T(128)}, f32[384,256]{1,0:T(8,128)S(1)}, s32[]{:T(128)}, f32[4,128,64]{2,1,0:T(8,128)S(1)}, ...), condition=%wide.region_13.14_spmd, body=%wide.region_12.13_spmd.sunk | while | flops 62947336 | bytes 1082027 | solution.py:73
  392.1 31.5 %all-gather.10 = f32[1024,128]{1,0:T(8,128)S(1)} all-gather(f32[128,128]{1,0:T(8,128)S(1)} %get-tuple-element.1838), channel_id=12, replica_groups=mesh['row'=8,'col'=4] {'row'}, dimensions={0}, use_global_device_ids=true | all-gather | bytes 589824 | tf_op jit(solution)/shard_map/all_gather | solution.py:38
  423.6 31.3 %all-gather.11 = f32[1024,128]{1,0:T(8,128)S(1)} all-gather(f32[128,128]{1,0:T(8,128)S(1)} %get-tuple-element.1837), channel_id=13, replica_groups=mesh['row'=8,'col'=4] {'row'}, dimensions={0}, use_global_device_ids=true | all-gather | bytes 589824 | tf_op jit(solution)/shard_map/all_gather | solution.py:38
  454.8 2.0 while.227
  457.1 1.5 collective-permute-start.16
  459.5 4.2 collective-permute-done.16
  463.7 12.4 %while.220 = (s32[]{:T(128)}, f32[384,256]{1,0:T(8,128)S(1)}, s32[]{:T(128)}, f32[4,128,64]{2,1,0:T(8,128)S(1)}, f32[4,64,64]{2,1,0:T(8,128)}, /*index=5*/s32[]{:T(128)}, s32[]{:T(128)}, s32[]{:T(128)}, s32[]{:T(128)}) while((s32[]{:T(128)}, f32[384,256]{1,0:T(8,128)S(1)}, s32[]{:T(128)}, f32[4,128,64]{2,1,0:T(8,128)S(1)}, ...), condition=%wide.region_17.18_spmd, body=%wide.region_16.17_spmd.sunk | while | flops 62947336 | bytes 1082027 | solution.py:73
  476.1 31.5 %all-gather.13 = f32[1024,128]{1,0:T(8,128)S(1)} all-gather(f32[128,128]{1,0:T(8,128)S(1)} %get-tuple-element.1836), channel_id=15, replica_groups=mesh['row'=8,'col'=4] {'row'}, dimensions={0}, use_global_device_ids=true | all-gather | bytes 589824 | tf_op jit(solution)/shard_map/all_gather | solution.py:38
  507.6 31.2 %all-gather.14 = f32[1024,128]{1,0:T(8,128)S(1)} all-gather(f32[128,128]{1,0:T(8,128)S(1)} %get-tuple-element.1835), channel_id=16, replica_groups=mesh['row'=8,'col'=4] {'row'}, dimensions={0}, use_global_device_ids=true | all-gather | bytes 589824 | tf_op jit(solution)/shard_map/all_gather | solution.py:38
  538.8 2.0 while.228
  541.1 1.3 collective-permute-start.20
  543.3 4.2 collective-permute-done.20
  547.5 12.4 %while.221 = (s32[]{:T(128)}, f32[384,256]{1,0:T(8,128)S(1)}, s32[]{:T(128)}, f32[4,128,64]{2,1,0:T(8,128)S(1)}, f32[4,64,64]{2,1,0:T(8,128)}, /*index=5*/s32[]{:T(128)}, s32[]{:T(128)}, s32[]{:T(128)}, s32[]{:T(128)}) while((s32[]{:T(128)}, f32[384,256]{1,0:T(8,128)S(1)}, s32[]{:T(128)}, f32[4,128,64]{2,1,0:T(8,128)S(1)}, ...), condition=%wide.region_21.22_spmd, body=%wide.region_20.21_spmd.sunk | while | flops 62947336 | bytes 1082027 | solution.py:73
  559.9 31.2 %all-gather.16 = f32[1024,128]{1,0:T(8,128)S(1)} all-gather(f32[128,128]{1,0:T(8,128)S(1)} %get-tuple-element.1834), channel_id=18, replica_groups=mesh['row'=8,'col'=4] {'row'}, dimensions={0}, use_global_device_ids=true | all-gather | bytes 589824 | tf_op jit(solution)/shard_map/all_gather | solution.py:38
  591.1 31.5 %all-gather.17 = f32[1024,128]{1,0:T(8,128)S(1)} all-gather(f32[128,128]{1,0:T(8,128)S(1)} %get-tuple-element.1833), channel_id=19, replica_groups=mesh['row'=8,'col'=4] {'row'}, dimensions={0}, use_global_device_ids=true | all-gather | bytes 589824 | tf_op jit(solution)/shard_map/all_gather | solution.py:38
  622.6 2.0 while.229
  624.9 1.3 collective-permute-start.24
  627.0 4.1 collective-permute-done.24
  631.2 12.3 %while.222 = (s32[]{:T(128)}, f32[384,256]{1,0:T(8,128)S(1)}, s32[]{:T(128)}, f32[4,128,64]{2,1,0:T(8,128)S(1)}, f32[4,64,64]{2,1,0:T(8,128)}, /*index=5*/s32[]{:T(128)}, s32[]{:T(128)}, s32[]{:T(128)}, s32[]{:T(128)}) while((s32[]{:T(128)}, f32[384,256]{1,0:T(8,128)S(1)}, s32[]{:T(128)}, f32[4,128,64]{2,1,0:T(8,128)S(1)}, ...), condition=%wide.region_25.26_spmd, body=%wide.region_24.25_spmd.sunk | while | flops 62947336 | bytes 1082027 | solution.py:73
  643.5 31.2 %all-gather.19 = f32[1024,128]{1,0:T(8,128)S(1)} all-gather(f32[128,128]{1,0:T(8,128)S(1)} %get-tuple-element.1832), channel_id=21, replica_groups=mesh['row'=8,'col'=4] {'row'}, dimensions={0}, use_global_device_ids=true | all-gather | bytes 589824 | tf_op jit(solution)/shard_map/all_gather | solution.py:38
  674.7 31.2 %all-gather.20 = f32[1024,128]{1,0:T(8,128)S(1)} all-gather(f32[128,128]{1,0:T(8,128)S(1)} %get-tuple-element.1831), channel_id=22, replica_groups=mesh['row'=8,'col'=4] {'row'}, dimensions={0}, use_global_device_ids=true | all-gather | bytes 589824 | tf_op jit(solution)/shard_map/all_gather | solution.py:38
  705.9 2.0 while.230
  708.2 1.3 collective-permute-start.28
  710.4 4.0 collective-permute-done.28
  714.4 8.9 %while.223 = (s32[]{:T(128)}, f32[384,256]{1,0:T(8,128)S(1)}, s32[]{:T(128)}, f32[4,128,64]{2,1,0:T(8,128)S(1)}, f32[4,64,64]{2,1,0:T(8,128)S(1)}, /*index=5*/s32[]{:T(128)}, s32[]{:T(128)}, s32[]{:T(128)}, s32[]{:T(128)}) while((s32[]{:T(128)}, f32[384,256]{1,0:T(8,128)S(1)}, s32[]{:T(128)}, f32[4,128,64]{2,1,0:T(8,128)S(1)}, ...), condition=%wide.region_29.30_spmd, body=%wide.region_28.29_spmd.sunk | while | flops 62947336 | bytes 1081519 | solution.py:73
  723.3 31.2 %all-gather.22 = f32[1024,128]{1,0:T(8,128)S(1)} all-gather(f32[128,128]{1,0:T(8,128)S(1)} %get-tuple-element.1830), channel_id=24, replica_groups=mesh['row'=8,'col'=4] {'row'}, dimensions={0}, use_global_device_ids=true | all-gather | bytes 589824 | tf_op jit(solution)/shard_map/all_gather | solution.py:38
  754.5 31.2 %all-gather.23 = f32[1024,128]{1,0:T(8,128)S(1)} all-gather(f32[128,128]{1,0:T(8,128)S(1)} %get-tuple-element.1829), channel_id=25, replica_groups=mesh['row'=8,'col'=4] {'row'}, dimensions={0}, use_global_device_ids=true | all-gather | bytes 589824 | tf_op jit(solution)/shard_map/all_gather | solution.py:38
  785.6 2.0 while.231
  (402 shorter events, 135.6 us)
Async XLA Ops:
  17.6 5.3 copy-start
  17.7 56.6 %collective-permute-start.1 = (f32[1,128,64]{2,1,0:T(8,128)S(1)}, f32[1,128,64]{2,1,0:T(8,128)}, u32[]{:S(2)}, u32[]{:S(2)}) collective-permute-start(f32[1,128,64]{2,1,0:T(8,128)S(1)} %bitcast.329), channel_id=1, source_target_pairs={{0,1},{1,2},{2,3},{3,0},{4,5},{5,6},{6,7},{7,4},{8,9},{9,10},{10,1... | collective-permute-start | bytes 98312 | tf_op jit(solution)/shard_map/ppermute | solution.py:18
  18.3 59.1 %collective-permute-start.2 = (f32[1,128,64]{2,1,0:T(8,128)S(1)}, f32[1,128,64]{2,1,0:T(8,128)}, u32[]{:S(2)}, u32[]{:S(2)}) collective-permute-start(f32[1,128,64]{2,1,0:T(8,128)S(1)} %bitcast.330), channel_id=1, source_target_pairs={{0,3},{1,0},{2,1},{3,2},{4,7},{5,4},{6,5},{7,6},{8,11},{9,8},{10,9... | collective-permute-start | bytes 98312 | tf_op jit(solution)/shard_map/ppermute | solution.py:23
  20.4 56.0 %collective-permute-start.5 = (f32[1,128,64]{2,1,0:T(8,128)S(1)}, f32[1,128,64]{2,1,0:T(8,128)}, u32[]{:S(2)}, u32[]{:S(2)}) collective-permute-start(f32[1,128,64]{2,1,0:T(8,128)S(1)} %bitcast.327), channel_id=1, source_target_pairs={{0,1},{1,2},{2,3},{3,0},{4,5},{5,6},{6,7},{7,4},{8,9},{9,10},{10,1... | collective-permute-start | bytes 98312 | tf_op jit(solution)/shard_map/ppermute | solution.py:18
  21.0 58.9 %collective-permute-start.6 = (f32[1,128,64]{2,1,0:T(8,128)S(1)}, f32[1,128,64]{2,1,0:T(8,128)}, u32[]{:S(2)}, u32[]{:S(2)}) collective-permute-start(f32[1,128,64]{2,1,0:T(8,128)S(1)} %bitcast.328), channel_id=1, source_target_pairs={{0,3},{1,0},{2,1},{3,2},{4,7},{5,4},{6,5},{7,6},{8,11},{9,8},{10,9... | collective-permute-start | bytes 98312 | tf_op jit(solution)/shard_map/ppermute | solution.py:23
  22.3 58.6 %collective-permute-start.9 = (f32[1,128,64]{2,1,0:T(8,128)S(1)}, f32[1,128,64]{2,1,0:T(8,128)}, u32[]{:S(2)}, u32[]{:S(2)}) collective-permute-start(f32[1,128,64]{2,1,0:T(8,128)S(1)} %bitcast.323), channel_id=1, source_target_pairs={{0,1},{1,2},{2,3},{3,0},{4,5},{5,6},{6,7},{7,4},{8,9},{9,10},{10,1... | collective-permute-start | bytes 98312 | tf_op jit(solution)/shard_map/ppermute | solution.py:18
  41.9 19.4 %copy-start.1 = (f32[1,1,128,64]{3,2,1,0:T(8,128)}, f32[1,1,128,64]{3,2,1,0:T(8,128)S(1)}, u32[]{:S(2)}) copy-start(f32[1,1,128,64]{3,2,1,0:T(8,128)S(1)} %copy.25) | copy-start | bytes 98308
  59.7 0.9 copy-start.3
  67.3 0.7 copy-start.5
  74.3 2.1 copy-start.2
  74.3 9.2 %collective-permute-start.10 = (f32[1,128,64]{2,1,0:T(8,128)S(1)}, f32[1,128,64]{2,1,0:T(8,128)S(1)}, u32[]{:S(2)}, u32[]{:S(2)}) collective-permute-start(f32[1,128,64]{2,1,0:T(8,128)S(1)} %bitcast.324), channel_id=1, source_target_pairs={{0,3},{1,0},{2,1},{3,2},{4,7},{5,4},{6,5},{7,6},{8,11},{9,8},{10,9... | collective-permute-start | bytes 98312 | tf_op jit(solution)/shard_map/ppermute | solution.py:23
  76.4 7.2 collective-permute-start.13
  77.4 8.9 %collective-permute-start.14 = (f32[1,128,64]{2,1,0:T(8,128)S(1)}, f32[1,128,64]{2,1,0:T(8,128)S(1)}, u32[]{:S(2)}, u32[]{:S(2)}) collective-permute-start(f32[1,128,64]{2,1,0:T(8,128)S(1)} %bitcast.334), channel_id=1, source_target_pairs={{0,3},{1,0},{2,1},{3,2},{4,7},{5,4},{6,5},{7,6},{8,11},{9,8},{10,9... | collective-permute-start | bytes 98312 | tf_op jit(solution)/shard_map/ppermute | solution.py:23
  80.0 6.3 collective-permute-start.17
  80.9 8.1 %collective-permute-start.18 = (f32[1,128,64]{2,1,0:T(8,128)S(1)}, f32[1,128,64]{2,1,0:T(8,128)S(1)}, u32[]{:S(2)}, u32[]{:S(2)}) collective-permute-start(f32[1,128,64]{2,1,0:T(8,128)S(1)} %bitcast.332), channel_id=1, source_target_pairs={{0,3},{1,0},{2,1},{3,2},{4,7},{5,4},{6,5},{7,6},{8,11},{9,8},{10,9... | collective-permute-start | bytes 98312 | tf_op jit(solution)/shard_map/ppermute | solution.py:23
  83.5 5.5 collective-permute-start.21
  83.6 8.1 %collective-permute-start.22 = (f32[1,128,64]{2,1,0:T(8,128)S(1)}, f32[1,128,64]{2,1,0:T(8,128)S(1)}, u32[]{:S(2)}, u32[]{:S(2)}) collective-permute-start(f32[1,128,64]{2,1,0:T(8,128)S(1)} %bitcast.326), channel_id=1, source_target_pairs={{0,3},{1,0},{2,1},{3,2},{4,7},{5,4},{6,5},{7,6},{8,11},{9,8},{10,9... | collective-permute-start | bytes 98312 | tf_op jit(solution)/shard_map/ppermute | solution.py:23
  86.2 6.8 collective-permute-start.25
  86.3 7.6 collective-permute-start.26
  88.9 5.9 collective-permute-start.29
  89.0 2.6 copy-start.4
  89.0 6.7 collective-permute-start.30
  91.7 6.2 collective-permute-start
  93.0 4.2 collective-permute-start.3
  93.9 94.9 %collective-permute-start.7 = (f32[1,128,64]{2,1,0:T(8,128)}, f32[1,128,64]{2,1,0:T(8,128)}, u32[]{:S(2)}, u32[]{:S(2)}) collective-permute-start(f32[1,128,64]{2,1,0:T(8,128)} %collective-permute-done.5), channel_id=1, source_target_pairs={{0,1},{1,2},{2,3},{3,0},{4,5},{5,6},{6,7},{7,4},{8,9},{9,10},{10,1... | collective-permute-start | bytes 98312 | tf_op jit(solution)/shard_map/ppermute | solution.py:18
  94.8 186.5 %collective-permute-start.11 = (f32[1,128,64]{2,1,0:T(8,128)}, f32[1,128,64]{2,1,0:T(8,128)}, u32[]{:S(2)}, u32[]{:S(2)}) collective-permute-start(f32[1,128,64]{2,1,0:T(8,128)} %collective-permute-done.9), channel_id=1, source_target_pairs={{0,1},{1,2},{2,3},{3,0},{4,5},{5,6},{6,7},{7,4},{8,9},{9,10},{10,1... | collective-permute-start | bytes 98312 | tf_op jit(solution)/shard_map/ppermute | solution.py:18
  95.7 277.8 %collective-permute-start.15 = (f32[1,128,64]{2,1,0:T(8,128)}, f32[1,128,64]{2,1,0:T(8,128)}, u32[]{:S(2)}, u32[]{:S(2)}) collective-permute-start(f32[1,128,64]{2,1,0:T(8,128)} %collective-permute-done.13), channel_id=1, source_target_pairs={{0,1},{1,2},{2,3},{3,0},{4,5},{5,6},{6,7},{7,4},{8,9},{9,10},{10,1... | collective-permute-start | bytes 98312 | tf_op jit(solution)/shard_map/ppermute | solution.py:18
  97.2 361.4 %collective-permute-start.19 = (f32[1,128,64]{2,1,0:T(8,128)}, f32[1,128,64]{2,1,0:T(8,128)}, u32[]{:S(2)}, u32[]{:S(2)}) collective-permute-start(f32[1,128,64]{2,1,0:T(8,128)} %collective-permute-done.17), channel_id=1, source_target_pairs={{0,1},{1,2},{2,3},{3,0},{4,5},{5,6},{6,7},{7,4},{8,9},{9,10},{10,1... | collective-permute-start | bytes 98312 | tf_op jit(solution)/shard_map/ppermute | solution.py:18
  97.8 444.6 %collective-permute-start.23 = (f32[1,128,64]{2,1,0:T(8,128)}, f32[1,128,64]{2,1,0:T(8,128)}, u32[]{:S(2)}, u32[]{:S(2)}) collective-permute-start(f32[1,128,64]{2,1,0:T(8,128)} %collective-permute-done.21), channel_id=1, source_target_pairs={{0,1},{1,2},{2,3},{3,0},{4,5},{5,6},{6,7},{7,4},{8,9},{9,10},{10,1... | collective-permute-start | bytes 98312 | tf_op jit(solution)/shard_map/ppermute | solution.py:18
  188.9 6.2 collective-permute-start.4
  195.0 431.2 %collective-permute-start.27 = (f32[1,128,64]{2,1,0:T(8,128)}, f32[1,128,64]{2,1,0:T(8,128)}, u32[]{:S(2)}, u32[]{:S(2)}) collective-permute-start(f32[1,128,64]{2,1,0:T(8,128)} %collective-permute-done.25), channel_id=1, source_target_pairs={{0,1},{1,2},{2,3},{3,0},{4,5},{5,6},{6,7},{7,4},{8,9},{9,10},{10,1... | collective-permute-start | bytes 98312 | tf_op jit(solution)/shard_map/ppermute | solution.py:18
  281.3 6.2 collective-permute-start.8
  287.4 422.1 %collective-permute-start.31 = (f32[1,128,64]{2,1,0:T(8,128)}, f32[1,128,64]{2,1,0:T(8,128)}, u32[]{:S(2)}, u32[]{:S(2)}) collective-permute-start(f32[1,128,64]{2,1,0:T(8,128)} %collective-permute-done.29), channel_id=1, source_target_pairs={{0,1},{1,2},{2,3},{3,0},{4,5},{5,6},{6,7},{7,4},{8,9},{9,10},{10,1... | collective-permute-start | bytes 98312 | tf_op jit(solution)/shard_map/ppermute | solution.py:18
  373.6 6.2 collective-permute-start.12
  457.1 6.5 collective-permute-start.16
  541.1 6.4 collective-permute-start.20
  624.9 6.2 collective-permute-start.24
  708.2 6.2 collective-permute-start.28
